TPU v7x, 32 devices: a whole 2x2x4 slice. The times are simulated.
32 devices in a mesh: seq: 8 (over z, y), tp: 4 (over x, core).
Axes of the slice: x: 2, y: 2, z: 4, core: 2. Of those that a mesh axis runs over, the one named last changes fastest.
Arguments:
- tokens: bfloat16 [4096, 2560], P('seq', 'tp'), may hold values from -6 to 6
- gate_weight: bfloat16 [2560, 5120], P(None, 'tp'), may hold values from -0.125 to 0.125
- inner_weight: bfloat16 [2560, 5120], P(None, 'tp'), may hold values from -0.125 to 0.125
- state_weight: bfloat16 [2560, 256], replicated, may hold values from -0.125 to 0.125
- step_weight: bfloat16 [2560, 80], P(None, 'tp'), may hold values from -0.125 to 0.125
- conv_inner: float32 [4, 5120], P(None, 'tp'), may hold values from -3 to 3
- conv_state: float32 [4, 256], replicated, may hold values from -3 to 3
- step_bias: float32 [80], P('tp'), may hold values from -3 to 1
- decay_rate: float32 [80], P('tp'), may hold values from 1e-05 to 0.02
- skip_gain: float32 [80], P('tp'), may hold values from 0.5 to 2
- norm_gain: float32 [5120], P('tp'), may hold values from 0.1 to 1.9
- out_weight: bfloat16 [5120, 2560], P('tp'), may hold values from -0.078125 to 0.078125
Outputs:
- layer_out: bfloat16 [4096, 2560], P(('seq', 'tp'))
All inputs are finite; a program needn't handle non-finite values.
Results may differ from a plain program's by a relative error of at most 0.018.
Values may be sent and summed in bfloat16 or wider, within the bound.
A program may use at most 128 MiB of HBM per device.

v0:
```python
import jax
import jax.numpy as jnp
from jax import lax
from jax.sharding import PartitionSpec as P

GROUP = 256
HIGHEST = lax.Precision.HIGHEST


def passed_along(shard, axis, by):
    size = lax.axis_size(axis)
    pairs = [(i, i + by) for i in range(size) if 0 <= i + by < size]
    return lax.ppermute(shard, axis, pairs)


def group_decay(inner_blk, inject_blk, step_blk, log_blk):
    cumulative = jnp.cumsum(log_blk, axis=0)
    ending = cumulative[-1]
    tail_weight = jnp.exp(ending[None, :] - cumulative) * step_blk
    scaled = inner_blk.astype(jnp.float32) * tail_weight[:, :, None]
    contribution = jnp.einsum(
        "thp,tn->hpn", scaled, inject_blk.astype(jnp.float32), precision=HIGHEST
    )
    return (cumulative, ending, contribution)


def group_intra(inner_blk, inject_blk, readout_blk, step_blk, cumulative):
    scores = jnp.dot(readout_blk, inject_blk.T, preferred_element_type=jnp.float32)
    length = scores.shape[0]
    causal = jnp.arange(length)[:, None] >= jnp.arange(length)[None, :]
    log_gaps = cumulative.T[:, :, None] - cumulative.T[:, None, :]
    decay_mask = jnp.exp(jnp.where(causal[None], log_gaps, -jnp.inf))
    mixing = (scores[None] * decay_mask * step_blk.T[:, None, :]).astype(jnp.bfloat16)
    return jnp.einsum("hts,shp->thp", mixing, inner_blk, preferred_element_type=jnp.float32)


def read_state(readout_blk, cumulative, carried):
    reads = jnp.einsum("tn,hpn->thp", readout_blk.astype(jnp.float32), carried, precision=HIGHEST)
    return reads * jnp.exp(cumulative)[:, :, None]


def fold_states(own_index, prefix, decay_all):
    own_prefix = lax.dynamic_index_in_dim(prefix, own_index, 0, keepdims=False)

    def absorb(carried, segment, first_row):
        row_count = segment.shape[0]
        positions = jnp.arange(row_count, dtype=jnp.int32)
        exponent = own_prefix[None, :] - prefix - decay_all
        factor = jnp.exp(jnp.where((positions < own_index)[:, None], exponent, -jnp.inf))
        return carried + jnp.einsum("kh,khpn->hpn", factor, segment, precision=HIGHEST)

    return absorb


def receive(decay_total, local_state):
    zero_state = jnp.zeros_like(local_state)
    decay_all = lax.all_gather(decay_total[None, :], "seq", axis=0, tiled=True)
    prefix = jnp.cumsum(decay_all, axis=0) - decay_all
    absorb = fold_states(lax.axis_index("seq"), prefix, decay_all)
    return absorb(
        zero_state,
        lax.all_gather(local_state[None].astype(jnp.bfloat16), "seq", axis=0, tiled=True).astype(
            jnp.float32
        ),
        jnp.int32(0),
    )


def on_device(
    tokens,
    gate_weight,
    inner_weight,
    state_weight,
    step_weight,
    conv_inner,
    conv_state,
    step_bias,
    decay_rate,
    skip_gain,
    norm_gain,
    out_weight,
):
    tok_rows = tokens.shape[0]
    weights = (gate_weight, inner_weight, state_weight, step_weight)
    segment = lax.all_gather(tokens, "tp", axis=1, tiled=True)
    gate_raw, inner_raw, state_raw, step_raw = tuple(
        (jnp.dot(segment, weight, preferred_element_type=jnp.float32) for weight in weights)
    )
    gate_act = gate_raw.astype(jnp.bfloat16)
    mixed_in = jnp.concatenate([inner_raw, state_raw], axis=1).astype(jnp.bfloat16)
    taps = conv_inner.shape[0]
    edge_rows = passed_along(mixed_in[tok_rows - (taps - 1) :], "seq", 1)
    padded = jnp.concatenate([edge_rows, mixed_in], axis=0)
    kernel = jnp.concatenate([conv_inner, conv_state], axis=1)
    conv_sum = jnp.zeros(mixed_in.shape, jnp.float32)
    for tap in range(taps):
        conv_sum = (
            conv_sum + padded[tap : tap + tok_rows].astype(jnp.float32) * kernel[tap][None, :]
        )
    conv_out = jax.nn.silu(conv_sum).astype(jnp.bfloat16)
    width_inner = inner_weight.shape[1]
    head_count = step_weight.shape[1]
    head_width = width_inner // head_count
    state_size = state_weight.shape[1] // 2
    inner_act = conv_out[:, :width_inner].reshape(tok_rows, head_count, head_width)
    inject = conv_out[:, width_inner : width_inner + state_size]
    readout = conv_out[:, width_inner + state_size :]
    time_step = jax.nn.softplus(step_raw + step_bias[None, :])
    log_decay = -time_step * decay_rate[None, :]
    block_count = tok_rows // GROUP
    pieces = []
    for group_number in range(block_count):
        row_span = slice(group_number * GROUP, (group_number + 1) * GROUP)
        pieces.append(
            (
                inner_act[row_span],
                inject[row_span],
                readout[row_span],
                time_step[row_span],
                log_decay[row_span],
            )
        )
    outputs = []
    local_state = jnp.zeros((head_count, head_width, state_size), jnp.float32)
    decay_total = jnp.zeros((head_count,), jnp.float32)
    summaries = []
    for group_number in range(block_count):
        inner_blk, inject_blk, readout_blk, step_blk, log_blk = pieces[group_number]
        cumulative, ending, contribution = group_decay(inner_blk, inject_blk, step_blk, log_blk)
        local_state = jnp.exp(ending)[:, None, None] * local_state + contribution
        decay_total = decay_total + ending
        summaries.append((cumulative, ending, contribution))
    carried = receive(decay_total, local_state)
    for group_number in range(block_count):
        inner_blk, inject_blk, readout_blk, step_blk, log_blk = pieces[group_number]
        cumulative, ending, contribution = summaries[group_number]
        block_out = group_intra(inner_blk, inject_blk, readout_blk, step_blk, cumulative)
        outputs.append(block_out + read_state(readout_blk, cumulative, carried))
        carried = jnp.exp(ending)[:, None, None] * carried + contribution
    ssd_out = jnp.concatenate(outputs, axis=0) + skip_gain[None, :, None] * inner_act.astype(
        jnp.float32
    )
    gated = ssd_out.reshape(tok_rows, width_inner) * jax.nn.silu(gate_act.astype(jnp.float32))
    square_total = lax.psum(jnp.sum(gated * gated, axis=1), "tp")
    mean_square = square_total / (width_inner * lax.axis_size("tp"))
    normed = (gated * lax.rsqrt(mean_square + 1e-05)[:, None] * norm_gain[None, :]).astype(
        jnp.bfloat16
    )
    return lax.psum_scatter(
        jnp.dot(normed, out_weight, preferred_element_type=jnp.float32).astype(jnp.bfloat16),
        "tp",
        scatter_dimension=0,
        tiled=True,
    )


def solution(mesh):
    in_specs = (
        P("seq", "tp"),
        P(None, "tp"),
        P(None, "tp"),
        P(),
        P(None, "tp"),
        P(None, "tp"),
        P(),
        P("tp"),
        P("tp"),
        P("tp"),
        P("tp"),
        P("tp", None),
    )
    out_specs = P(("seq", "tp"), None)
    return jax.shard_map(
        on_device, mesh=mesh, in_specs=in_specs, out_specs=out_specs, check_vma=False
    )
```

profile of v0, /device:TPU:0, one launch (start us, length us, event | category | flops | bytes accessed | tf_op | source)
XLA Modules:
  0.0 202.1 jit_solution(8216762679849479591)
XLA Ops:
  6.5 0.7 all-gather.5.cloned.1.call-update
  7.3 0.7 constant_dynamic-update-slice_fusion.1
  8.0 0.7 constant_dynamic-update-slice_fusion
  8.8 28.4 %all-gather.5.cloned.1.call-done = bf16[512,2560]{1,0:T(8,128)(2,1)} async-done(((bf16[512,640]{1,0:T(8,128)(2,1)}), bf16[512,2560]{1,0:T(8,128)(2,1)}) %all-gather.5.cloned.1.call-update) | async-done | bytes 2621456 | tf_op jit(solution)/shard_map/all_gather | solution.py:85
  37.2 2.6 %negate_multiply_fusion = (f32[512,20]{0,1:T(8,128)S(1)}, f32[512,20]{0,1:T(8,128)S(1)}) fusion(f32[20]{0:T(128)} %param.20, f32[20]{0:T(128)} %param.19, bf16[512,2560]{1,0:T(8,128)(2,1)} %all-gather.5.cloned.1.call-done, bf16[2560,20]{0,1:T(8,128)(2,1)} %param.16), kind=kOutput, calls=%fused_computation.74 | convolution fusion | flops 52520960 | bytes 2805920 | tf_op jit(solution)/shard_map/dot_general | solution.py:87
  41.8 7.3 %convolution_convert_fusion.2 = bf16[512,1280]{1,0:T(8,128)(2,1)S(1)} fusion(bf16[512,2560]{1,0:T(8,128)(2,1)} %all-gather.5.cloned.1.call-done, bf16[2560,1280]{1,0:T(8,128)(2,1)} %param.14), kind=kOutput, calls=%fused_computation.7 | convolution fusion | flops 3356098560 | bytes 10485760 | tf_op jit(solution)/shard_map/dot_general | solution.py:87
  49.2 0.8 convolution_convert_fusion.3
  50.0 3.4 %collective-permute-start = (bf16[3,1536]{1,0:T(4,128)(2,1)S(1)}, bf16[3,1536]{1,0:T(4,128)(2,1)S(1)}, u32[]{:S(2)}, u32[]{:S(2)}) collective-permute-start(bf16[3,1536]{1,0:T(4,128)(2,1)S(1)} %fusion.57), channel_id=1, source_target_pairs={{0,4},{4,8},{8,12},{12,16},{16,20},{20,24},{24,28},{1,5},{5,9},{9,... | collective-permute-start | bytes 27656 | tf_op jit(solution)/shard_map/ppermute | solution.py:13
  53.6 0.7 slice_bitcast_fusion.3
  55.3 2.0 multiply_convert_fusion.2
  57.2 0.9 fusion.60
  58.2 2.2 %copy.34 = bf16[256,1280]{0,1:T(8,128)(2,1)} copy(bf16[256,1280]{1,0:T(8,128)(2,1)} %get-tuple-element.12) | data formatting | bytes 1310720 | tf_op jit(solution)/shard_map/slice | solution.py:116
  60.3 1.1 copy.39
  61.4 1.9 fusion.29
  63.3 2.6 %fusion.35 = bf16[20,64,128]{2,1,0:T(8,128)(2,1)} fusion(bf16[256,20,64]{0,2,1:T(8,128)(2,1)} %bitcast.69, f32[256,20]{0,1:T(8,128)} %get-tuple-element.17, f32[20,64,128]{2,1,0:T(8,128)S(1)} %fusion.29, f32[20]{0:T(128)S(1)} %get-tuple-element.23, f32[20]{0:T(128)S(1)} %exp.52, bf16[512,1536]{1,0:T(8,128)(2,1)S(1)} %multiply_convert_fusion.2), kind=kOutput, calls=%fused_computation.50 | convolution fusion | flops 504627200 | bytes 1725440 | tf_op jit(solution)/shard_map/thp,tn->hpn/dot_general | solution.py:21
  66.0 0.7 mul.225
  66.7 0.7 mul.226
  67.4 0.6 iota_compare_fusion
  68.0 21.5 %all-gather.1 = f32[8,1,20]{2,1,0:T(1,128)S(1)} all-gather(f32[1,1,20]{2,1,0:T(1,128)S(1)} %bitcast.84), channel_id=1, replica_groups=mesh['seq'=8,'tp'=4] {'seq'}, dimensions={0}, use_global_device_ids=true | all-gather | bytes 720 | tf_op jit(solution)/shard_map/all_gather | solution.py:57
  90.2 3.9 %fusion.21 = f32[256,20,64]{0,2,1:T(8,128)} fusion(bf16[256,20,64]{0,2,1:T(8,128)(2,1)} %bitcast.72, f32[20,256]{1,0:T(8,128)} %get-tuple-element.14, f32[20,256]{1,0:T(8,128)} %bitcast.75, f32[256,256]{1,0:T(8,128)S(1)} %fusion.53, pred[256,256]{1,0:T(8,128)(4,1)} %iota_compare_fusion), kind=kOutput, calls=%fused_computation.36 | convolution fusion | flops 174325760 | bytes 2334720 | tf_op jit(solution)/shard_map/hts,shp->thp/dot_general | solution.py:34
  94.1 2.7 %fusion.20 = f32[256,20,64]{0,2,1:T(8,128)} fusion(bf16[256,20,64]{0,2,1:T(8,128)(2,1)S(1)} %bitcast.70, f32[20,256]{1,0:T(8,128)S(1)} %copy-done.10, f32[20,256]{1,0:T(8,128)S(1)} %bitcast.78, f32[256,256]{1,0:T(8,128)S(1)} %fusion.48, pred[256,256]{1,0:T(8,128)(4,1)S(1)} %copy-done.9), kind=kOutput, calls=%fused_computation.35 | convolution fusion | flops 174325760 | bytes 2334720 | tf_op jit(solution)/shard_map/hts,shp->thp/dot_general | solution.py:34
  96.9 24.3 %all-gather.7.cloned.1.call-done = bf16[160,64,128]{2,1,0:T(8,128)(2,1)} async-done(((bf16[20,64,128]{2,1,0:T(8,128)(2,1)}), bf16[160,64,128]{2,1,0:T(8,128)(2,1)}) %all-gather.7.cloned.1.call-update) | async-done | bytes 2621456 | tf_op jit(solution)/shard_map/all_gather | solution.py:62
  121.2 5.0 %fusion.6 = f32[20,1,64,128]{3,1,2,0:T(1,128)S(1)} fusion(f32[8,20,1,1]{0,2,3,1:T(1,128)S(1)} %copy.43, bf16[8,20,64,128]{3,2,1,0:T(8,128)(2,1)} %bitcast.68), kind=kOutput, calls=%fused_computation.15 | convolution fusion | flops 15728640 | bytes 3277440 | tf_op jit(solution)/shard_map/kh,khpn->hpn/dot_general | solution.py:50
  126.2 0.8 copy-done.1
  127.0 1.8 fusion.22
  128.8 2.8 %copy.40 = f32[256,1280]{1,0:T(8,128)} copy(f32[256,1280]{0,1:T(8,128)} %bitcast.66) | data formatting | bytes 2621440 | tf_op jit(solution)/shard_map/concatenate | solution.py:140
  131.6 3.3 %fusion.23 = f32[256,20,64]{0,2,1:T(8,128)} fusion(f32[256,20,64]{0,2,1:T(8,128)} %fusion.20, f32[256,20]{0,1:T(8,128)} %get-tuple-element.20, f32[20,64,128]{2,1,0:T(8,128)S(1)} %fusion.29, f32[20,64,128]{2,1,0:T(8,128)} %bitcast.65, f32[20]{0:T(128)S(1)} %copy-done.12, bf16[512,1536]{1,0:T(8,128)(2,1)S(1)} %multiply_convert_fusion.2), kind=kOutput, calls=%fused_computation.40 | convolution fusion | flops 504299520 | bytes 4018688 | tf_op jit(solution)/shard_map/tn,hpn->thp/dot_general | solution.py:38
  134.9 2.9 %copy.41 = f32[256,1280]{1,0:T(8,128)} copy(f32[256,1280]{0,1:T(8,128)} %bitcast.67) | data formatting | bytes 2621440 | tf_op jit(solution)/shard_map/concatenate | solution.py:140
  137.8 9.8 %multiply_reduce_fusion = (f32[512]{0:T(512)S(1)}, f32[512,1280]{1,0:T(8,128)}) fusion(bf16[512,2560]{1,0:T(8,128)(2,1)} %all-gather.5.cloned.1.call-done, bf16[2560,1280]{1,0:T(8,128)(2,1)} %param.13, bf16[512,1536]{1,0:T(8,128)(2,1)S(1)} %multiply_convert_fusion.2, f32[1280]{0:T(1024)S(1)} %copy-done.11, f32[256,1280]{1,0:T(8,128)} %copy.41, ...), kind=kOutput, calls=%fused_computation.18 | convolution fusion | flops 3363962368 | bytes 15735808 | tf_op jit(solution)/shard_map/dot_general | solution.py:87
  147.6 5.6 %psum.7 = f32[512]{0:T(512)S(1)} all-reduce(f32[512]{0:T(512)S(1)} %get-tuple-element.26), channel_id=1, replica_groups=mesh['seq'=8,'tp'=4] {'tp'}, use_global_device_ids=true, to_apply=%region_6.7 | all-reduce | flops 512 | bytes 4096 | tf_op jit(solution)/shard_map/psum | solution.py:144
  153.3 8.8 %convolution_convert_fusion = bf16[512,2560]{1,0:T(8,128)(2,1)} fusion(bf16[1280,2560]{1,0:T(8,128)(2,1)} %param.23, f32[512,1280]{1,0:T(8,128)} %get-tuple-element.27, f32[1280]{0:T(1024)S(1)} %copy-done.13, f32[512]{0:T(512)S(1)} %add_rsqrt_fusion), kind=kOutput, calls=%fused_computation.2 | convolution fusion | flops 3358720000 | bytes 11803648 | tf_op jit(solution)/shard_map/dot_general | solution.py:150
  162.1 33.5 %reduce-scatter.2.cloned.1.call-done = bf16[128,2560]{1,0:T(8,128)(2,1)} async-done(((bf16[512,2560]{1,0:T(8,128)(2,1)}), bf16[128,2560]{1,0:T(8,128)(2,1)}) %reduce-scatter.2.cloned.1.call-update) | async-done | bytes 655376 | tf_op jit(solution)/shard_map/reduce_scatter | solution.py:149
  (69 shorter events, 3.8 us)
Async XLA Ops:
  6.5 42.6 %copy-start = (bf16[2560,256]{1,0:T(8,128)(2,1)S(1)}, bf16[2560,256]{1,0:T(8,128)(2,1)}, u32[]{:S(2)}) copy-start(bf16[2560,256]{1,0:T(8,128)(2,1)} %param.15) | copy-start | bytes 3932164
  6.5 30.6 %all-gather.5.cloned.1.call-start = ((), (), s32[]{:S(2)}) async-start(), calls=%async_computation.1 | async-start | bytes 3276800 | tf_op jit(solution)/shard_map/all_gather | solution.py:85
  7.3 113.9 %all-gather.7.cloned.1.call-start = ((), (), s32[]{:S(2)}) async-start(), calls=%async_computation.3 | async-start | bytes 2949120 | tf_op jit(solution)/shard_map/all_gather | solution.py:62
  40.8 12.8 %copy-start.5 = (f32[3,8,2,128]{3,1,2,0:T(8,128)}, f32[3,8,2,128]{3,1,2,0:T(8,128)S(1)}, u32[]{:S(2)}) copy-start(f32[3,8,2,128]{3,1,2,0:T(8,128)S(1)} %copy.46) | copy-start | bytes 73732
  41.8 11.9 %copy-start.6 = (f32[3,8,2,128]{3,1,2,0:T(8,128)}, f32[3,8,2,128]{3,1,2,0:T(8,128)S(1)}, u32[]{:S(2)}) copy-start(f32[3,8,2,128]{3,1,2,0:T(8,128)S(1)} %copy.47) | copy-start | bytes 73732
  41.8 7.4 %copy-start.3 = (bf16[512,2560]{1,0:T(8,128)(2,1)S(1)}, bf16[512,2560]{1,0:T(8,128)(2,1)}, u32[]{:S(2)}) copy-start(bf16[512,2560]{1,0:T(8,128)(2,1)} %all-gather.5.cloned.1.call-done) | copy-start | bytes 7864324
  50.0 4.9 %collective-permute-start = (bf16[3,1536]{1,0:T(4,128)(2,1)S(1)}, bf16[3,1536]{1,0:T(4,128)(2,1)S(1)}, u32[]{:S(2)}, u32[]{:S(2)}) collective-permute-start(bf16[3,1536]{1,0:T(4,128)(2,1)S(1)} %fusion.57), channel_id=1, source_target_pairs={{0,4},{4,8},{8,12},{12,16},{16,20},{20,24},{24,28},{1,5},{5,9},{9,... | collective-permute-start | bytes 27656 | tf_op jit(solution)/shard_map/ppermute | solution.py:13
  65.9 129.7 %reduce-scatter.2.cloned.1.call-start = ((), (), s32[]{:S(2)}) async-start(), calls=%async_computation.2 | async-start | bytes 3276800 | tf_op jit(solution)/shard_map/reduce_scatter | solution.py:149
  90.1 4.0 %copy-start.2 = (bf16[256,1280]{0,1:T(8,128)(2,1)S(1)}, bf16[256,1280]{0,1:T(8,128)(2,1)}, u32[]{:S(2)}) copy-start(bf16[256,1280]{0,1:T(8,128)(2,1)} %copy.39) | copy-start | bytes 1966084
  90.1 4.0 %copy-start.7 = (f32[3,8,2,128]{3,1,2,0:T(8,128)S(1)}, f32[3,8,2,128]{3,1,2,0:T(8,128)}, u32[]{:S(2)}) copy-start(f32[3,8,2,128]{3,1,2,0:T(8,128)} %copy-done.6) | copy-start | bytes 73732
  90.1 4.0 %copy-start.9 = (pred[256,256]{1,0:T(8,128)(4,1)S(1)}, pred[256,256]{1,0:T(8,128)(4,1)}, u32[]{:S(2)}) copy-start(pred[256,256]{1,0:T(8,128)(4,1)} %iota_compare_fusion) | copy-start | bytes 196612
  90.2 4.0 %copy-start.10 = (f32[20,256]{1,0:T(8,128)S(1)}, f32[20,256]{1,0:T(8,128)}, u32[]{:S(2)}) copy-start(f32[20,256]{1,0:T(8,128)} %get-tuple-element.16) | copy-start | bytes 61444
  121.2 5.8 %copy-start.4 = (f32[256,20,64]{0,2,1:T(8,128)S(1)}, f32[256,20,64]{0,2,1:T(8,128)}, u32[]{:S(2)}) copy-start(f32[256,20,64]{0,2,1:T(8,128)} %fusion.21) | copy-start | bytes 3932164
  121.2 5.8 %copy-start.8 = (f32[256,20]{0,1:T(8,128)S(1)}, f32[256,20]{0,1:T(8,128)}, u32[]{:S(2)}) copy-start(f32[256,20]{0,1:T(8,128)} %get-tuple-element.21) | copy-start | bytes 61444
  126.2 0.8 copy-start.1
  127.0 4.6 %copy-start.12 = (f32[20]{0:T(128)S(1)}, f32[20]{0:T(128)}, u32[]{:S(2)}) copy-start(f32[20]{0:T(128)} %get-tuple-element.22) | copy-start | bytes 244
  131.6 6.2 %copy-start.11 = (f32[1280]{0:T(1024)S(1)}, f32[1280]{0:T(1024)}, u32[]{:S(2)}) copy-start(f32[1280]{0:T(1024)} %mul.226) | copy-start | bytes 15364
  137.8 15.5 %copy-start.13 = (f32[1280]{0:T(1024)S(1)}, f32[1280]{0:T(1024)}, u32[]{:S(2)}) copy-start(f32[1280]{0:T(1024)} %param.22) | copy-start | bytes 15364
Sparse Core Ops, SparseCore 0:
  8.9 28.2 all-gather.4
  66.0 55.1 all-gather.6
  162.2 33.3 reduce-scatter.1
where the time goes:
time: 203 us; the launch traced here: 202 us
  waiting for transfers between devices  86.9 us (43%)
  matrix products  51 us (25%)
  blocking collectives  27.2 us (13%)
  local copies, waits for them, and re-layouts  14.2 us (7%)
  between operations  13.4 us (7%)
  other arithmetic  5.98 us (3%)
  starting transfers between devices  3.46 us (2%)
    reduce_scatter x1, waiting for transfers between devices, on_device(): lax.psum_scatter(jnp.dot(normed, out_weight, preferred_element_type=jnp.f...  33.5 us
    all_gather x1, waiting for transfers between devices, on_device(): segment = lax.all_gather(tokens, 'tp', axis=1, tiled=True)  28.4 us
    all_gather x1, waiting for transfers between devices, receive(): lax.all_gather(local_state[None].astype(jnp.bfloat16), 'seq', axis=0, til...  24.3 us
    all_gather x1, blocking collectives, receive(): decay_all = lax.all_gather(decay_total[None, :], 'seq', axis=0, tiled=True)  21.5 us
    dot_general x4, matrix products, on_device(): jnp.dot(segment, weight, preferred_element_type=jnp.float32)  20.7 us
    dot_general x1, matrix products, on_device(): jnp.dot(normed, out_weight, preferred_element_type=jnp.float32)  8.79 us
    dot_general x2, matrix products, group_intra(): jnp.einsum('hts,shp->thp', mixing, inner_blk, preferred_element_type=jnp....  6.67 us
    concatenate x2, local copies, waits for them, and re-layouts, on_device(): jnp.concatenate(outputs, axis=0)  5.7 us
  transfers between devices with their start and end apart: 4, of which 3 were waited for; matrix products, arithmetic and copies ran while one was open for 6% of the time, Pallas kernels for 0%

commit v1 on v0

--- a/solution.py
+++ b/solution.py
@@ -5,6 +5,16 @@
 
 GROUP = 256
 HIGHEST = lax.Precision.HIGHEST
+
+
+def pass_along(array, axis, dim):
+    peers = lax.axis_size(axis)
+    held, blocks = (array, [array])
+    for _ in range(peers - 1):
+        held = lax.ppermute(held, axis, [(i, (i + 1) % peers) for i in range(peers)])
+        blocks.insert(0, held)
+    line = jnp.concatenate(blocks, axis=dim)
+    return jnp.roll(line, (lax.axis_index(axis) + 1) * array.shape[dim], axis=dim)
 
 
 def passed_along(shard, axis, by):
@@ -82,7 +92,7 @@
 ):
     tok_rows = tokens.shape[0]
     weights = (gate_weight, inner_weight, state_weight, step_weight)
-    segment = lax.all_gather(tokens, "tp", axis=1, tiled=True)
+    segment = pass_along(tokens, "tp", 1)
     gate_raw, inner_raw, state_raw, step_raw = tuple(
         (jnp.dot(segment, weight, preferred_element_type=jnp.float32) for weight in weights)
     )

time: 203 us -> 210 us (1.034)
  local copies, waits for them, and re-layouts: 14.2 us -> 19.8 us
    ppermute x0 -> x3, waiting for transfers between devices: none -> 29 us  [pass_along(): lax.ppermute(held, axis, [(i, (i + 1) % peers) for i in range(peers)])]
    all_gather x1 -> x0, waiting for transfers between devices: 28.4 us -> none  [on_device(): segment = lax.all_gather(tokens, 'tp', axis=1, tiled=True)]
    unnamed x33 -> x52, local copies, waits for them, and re-layouts: 1.64 us -> 7.15 us
  transfers between devices with their start and end apart: 4 -> 6, of which waited for: 3 -> 5; matrix products, arithmetic and copies ran while one was open for 6% -> 6% of each run, Pallas kernels for 0% -> 0%
where the time goes in v1:
time: 210 us
  waiting for transfers between devices  87.8 us (42%)
  matrix products  50.3 us (24%)
  blocking collectives  27.5 us (13%)
  local copies, waits for them, and re-layouts  19.8 us (9%)
  between operations  13.8 us (7%)
  other arithmetic  5.98 us (3%)
  starting transfers between devices  4.76 us (2%)
    reduce_scatter x1, waiting for transfers between devices, on_device(): lax.psum_scatter(jnp.dot(normed, out_weight, preferred_element_type=jnp.f...  33.5 us
    ppermute x3, waiting for transfers between devices, pass_along(): lax.ppermute(held, axis, [(i, (i + 1) % peers) for i in range(peers)])  29 us
    all_gather x1, waiting for transfers between devices, receive(): lax.all_gather(local_state[None].astype(jnp.bfloat16), 'seq', axis=0, til...  25.2 us
    all_gather x1, blocking collectives, receive(): decay_all = lax.all_gather(decay_total[None, :], 'seq', axis=0, tiled=True)  21.9 us
    dot_general x4, matrix products, on_device(): jnp.dot(segment, weight, preferred_element_type=jnp.float32)  19.9 us
    dot_general x1, matrix products, on_device(): jnp.dot(normed, out_weight, preferred_element_type=jnp.float32)  8.78 us
    unnamed x52, local copies, waits for them, and re-layouts  7.15 us
    dot_general x2, matrix products, group_intra(): jnp.einsum('hts,shp->thp', mixing, inner_blk, preferred_element_type=jnp....  6.67 us
  transfers between devices with their start and end apart: 6, of which 5 were waited for; matrix products, arithmetic and copies ran while one was open for 6% of the time, Pallas kernels for 0%

profile of v1, /device:TPU:0, one launch (start us, length us, event | category | flops | bytes accessed | tf_op | source)
XLA Modules:
  0.0 209.9 jit_solution(1927954254855941617)
XLA Ops:
  7.0 10.4 %collective-permute-done = bf16[512,640]{1,0:T(8,128)(2,1)S(1)} collective-permute-done((bf16[512,640]{1,0:T(8,128)(2,1)}, bf16[512,640]{1,0:T(8,128)(2,1)S(1)}, u32[]{:S(2)}, u32[]{:S(2)}) %collective-permute-start) | collective-permute-done | bytes 655392 | tf_op jit(solution)/shard_map/ppermute | solution.py:14
  17.5 10.0 %collective-permute-done.1 = bf16[512,640]{1,0:T(8,128)(2,1)S(1)} collective-permute-done((bf16[512,640]{1,0:T(8,128)(2,1)S(1)}, bf16[512,640]{1,0:T(8,128)(2,1)S(1)}, u32[]{:S(2)}, u32[]{:S(2)}) %collective-permute-start.1) | collective-permute-done | bytes 655392 | tf_op jit(solution)/shard_map/ppermute | solution.py:14
  27.5 0.7 constant_dynamic-update-slice_fusion.9
  29.0 8.6 %collective-permute-done.2 = bf16[512,640]{1,0:T(8,128)(2,1)} collective-permute-done((bf16[512,640]{1,0:T(8,128)(2,1)S(1)}, bf16[512,640]{1,0:T(8,128)(2,1)}, u32[]{:S(2)}, u32[]{:S(2)}) %collective-permute-start.2) | collective-permute-done | bytes 655392 | tf_op jit(solution)/shard_map/ppermute | solution.py:14
  37.6 1.2 constant_dynamic-update-slice_fusion.7
  39.3 1.3 constant_dynamic-update-slice_fusion.3
  41.0 2.3 %copy-done.4 = bf16[512,5120]{1,0:T(8,128)(2,1)} copy-done((bf16[512,5120]{1,0:T(8,128)(2,1)}, bf16[512,5120]{1,0:T(8,128)(2,1)S(1)}, u32[]{:S(2)}) %copy-start.4) | copy-done | bytes 5242904
  43.3 1.2 negate_multiply_fusion
  46.5 7.5 %convolution_convert_fusion.2 = bf16[512,1280]{1,0:T(8,128)(2,1)S(1)} fusion(bf16[2560,1280]{1,0:T(8,128)(2,1)} %param.14, bf16[512,5120]{1,0:T(8,128)(2,1)} %copy-done.4, s32[]{:T(128)S(6)} %select_n.33), kind=kOutput, calls=%fused_computation.7 | convolution fusion | flops 3356098560 | bytes 10485764 | tf_op jit(solution)/shard_map/dot_general | solution.py:97
  54.0 1.2 fusion.44
  55.2 4.2 %collective-permute-start.3 = (bf16[3,1536]{1,0:T(4,128)(2,1)S(1)}, bf16[3,1536]{1,0:T(4,128)(2,1)S(1)}, u32[]{:S(2)}, u32[]{:S(2)}) collective-permute-start(bf16[3,1536]{1,0:T(4,128)(2,1)S(1)} %fusion.71), channel_id=1, source_target_pairs={{0,4},{4,8},{8,12},{12,16},{16,20},{20,24},{24,28},{1,5},{5,9},{9,... | collective-permute-start | bytes 27656 | tf_op jit(solution)/shard_map/ppermute | solution.py:23
  59.7 0.7 slice_bitcast_fusion.3
  61.3 2.0 multiply_convert_fusion.2
  63.3 0.9 fusion.78
  64.2 2.2 %copy.34 = bf16[256,1280]{0,1:T(8,128)(2,1)} copy(bf16[256,1280]{1,0:T(8,128)(2,1)} %get-tuple-element.12) | data formatting | bytes 1310720 | tf_op jit(solution)/shard_map/slice | solution.py:126
  66.4 1.1 copy.39
  67.5 1.9 fusion.35
  69.3 2.6 %fusion.41 = bf16[20,64,128]{2,1,0:T(8,128)(2,1)} fusion(bf16[256,20,64]{0,2,1:T(8,128)(2,1)} %bitcast.65, f32[256,20]{0,1:T(8,128)} %get-tuple-element.17, f32[20,64,128]{2,1,0:T(8,128)S(1)} %fusion.35, f32[20]{0:T(128)S(1)} %get-tuple-element.23, f32[20]{0:T(128)S(1)} %exp.52, bf16[512,1536]{1,0:T(8,128)(2,1)S(1)} %multiply_convert_fusion.2), kind=kOutput, calls=%fused_computation.56 | convolution fusion | flops 504627200 | bytes 1725440 | tf_op jit(solution)/shard_map/thp,tn->hpn/dot_general | solution.py:31
  74.1 21.9 %all-gather.1 = f32[8,1,20]{2,1,0:T(1,128)S(1)} all-gather(f32[1,1,20]{2,1,0:T(1,128)S(1)} %bitcast.82), channel_id=1, replica_groups=mesh['seq'=8,'tp'=4] {'seq'}, dimensions={0}, use_global_device_ids=true | all-gather | bytes 720 | tf_op jit(solution)/shard_map/all_gather | solution.py:67
  96.6 3.9 %fusion.27 = f32[256,20,64]{0,2,1:T(8,128)} fusion(bf16[256,20,64]{0,2,1:T(8,128)(2,1)} %bitcast.68, f32[20,256]{1,0:T(8,128)} %get-tuple-element.14, f32[20,256]{1,0:T(8,128)} %bitcast.76, f32[256,256]{1,0:T(8,128)S(1)} %fusion.65, pred[256,256]{1,0:T(8,128)(4,1)} %iota_compare_fusion), kind=kOutput, calls=%fused_computation.42 | convolution fusion | flops 174325760 | bytes 2334720 | tf_op jit(solution)/shard_map/hts,shp->thp/dot_general | solution.py:44
  100.5 2.8 %fusion.26 = f32[256,20,64]{0,2,1:T(8,128)} fusion(bf16[256,20,64]{0,2,1:T(8,128)(2,1)S(1)} %bitcast.66, f32[20,256]{1,0:T(8,128)S(1)} %copy-done.12, f32[20,256]{1,0:T(8,128)S(1)} %bitcast.73, f32[256,256]{1,0:T(8,128)S(1)} %fusion.60, pred[256,256]{1,0:T(8,128)(4,1)S(1)} %copy-done.11), kind=kOutput, calls=%fused_computation.41 | convolution fusion | flops 174325760 | bytes 2334720 | tf_op jit(solution)/shard_map/hts,shp->thp/dot_general | solution.py:44
  103.3 25.2 %all-gather.4.cloned.1.call-done = bf16[160,64,128]{2,1,0:T(8,128)(2,1)} async-done(((bf16[20,64,128]{2,1,0:T(8,128)(2,1)}), bf16[160,64,128]{2,1,0:T(8,128)(2,1)}) %all-gather.4.cloned.1.call-update) | async-done | bytes 2621456 | tf_op jit(solution)/shard_map/all_gather | solution.py:72
  128.5 5.0 %fusion.6 = f32[20,1,64,128]{3,1,2,0:T(1,128)S(1)} fusion(f32[8,20,1,1]{0,2,3,1:T(1,128)S(1)} %copy.43, bf16[8,20,64,128]{3,2,1,0:T(8,128)(2,1)} %bitcast.64), kind=kOutput, calls=%fused_computation.15 | convolution fusion | flops 15728640 | bytes 3277440 | tf_op jit(solution)/shard_map/kh,khpn->hpn/dot_general | solution.py:60
  133.5 0.8 copy-done.1
  134.3 1.8 fusion.28
  136.1 2.9 %copy.40 = f32[256,1280]{1,0:T(8,128)} copy(f32[256,1280]{0,1:T(8,128)} %bitcast.62) | data formatting | bytes 2621440 | tf_op jit(solution)/shard_map/concatenate | solution.py:150
  139.0 3.3 %fusion.29 = f32[256,20,64]{0,2,1:T(8,128)} fusion(f32[256,20,64]{0,2,1:T(8,128)} %fusion.26, f32[256,20]{0,1:T(8,128)} %get-tuple-element.20, f32[20,64,128]{2,1,0:T(8,128)S(1)} %fusion.35, f32[20,64,128]{2,1,0:T(8,128)} %bitcast.61, f32[20]{0:T(128)S(1)} %copy-done.16, bf16[512,1536]{1,0:T(8,128)(2,1)S(1)} %multiply_convert_fusion.2), kind=kOutput, calls=%fused_computation.46 | convolution fusion | flops 504299520 | bytes 4018688 | tf_op jit(solution)/shard_map/tn,hpn->thp/dot_general | solution.py:48
  142.3 2.8 %copy.41 = f32[256,1280]{1,0:T(8,128)} copy(f32[256,1280]{0,1:T(8,128)} %bitcast.63) | data formatting | bytes 2621440 | tf_op jit(solution)/shard_map/concatenate | solution.py:150
  145.1 10.1 %multiply_reduce_fusion = (f32[512]{0:T(512)S(1)}, f32[512,1280]{1,0:T(8,128)}) fusion(bf16[2560,1280]{1,0:T(8,128)(2,1)} %param.13, bf16[512,5120]{1,0:T(8,128)(2,1)} %copy-done.4, s32[]{:T(128)S(6)} %select_n.33, bf16[512,1536]{1,0:T(8,128)(2,1)S(1)} %multiply_convert_fusion.2, f32[1280]{0:T(1024)S(1)} %copy-done.13, f32[256,1280]{1,0:T(8,128)} %copy.41, ...), kind=kOutput, calls=%fused_computation.18 | convolution fusion | flops 3363962368 | bytes 15735812 | tf_op jit(solution)/shard_map/dot_general | solution.py:97
  155.2 5.6 %psum.7 = f32[512]{0:T(512)S(1)} all-reduce(f32[512]{0:T(512)S(1)} %get-tuple-element.26), channel_id=1, replica_groups=mesh['seq'=8,'tp'=4] {'tp'}, use_global_device_ids=true, to_apply=%region_6.7 | all-reduce | flops 512 | bytes 4096 | tf_op jit(solution)/shard_map/psum | solution.py:154
  160.8 8.8 %convolution_convert_fusion = bf16[512,2560]{1,0:T(8,128)(2,1)} fusion(bf16[1280,2560]{1,0:T(8,128)(2,1)} %param.23, f32[512,1280]{1,0:T(8,128)} %get-tuple-element.27, f32[1280]{0:T(1024)S(1)} %copy-done.17, f32[512]{0:T(512)S(1)} %add_rsqrt_fusion), kind=kOutput, calls=%fused_computation.2 | convolution fusion | flops 3358720000 | bytes 11803648 | tf_op jit(solution)/shard_map/dot_general | solution.py:160
  169.6 33.5 %reduce-scatter.2.cloned.1.call-done = bf16[128,2560]{1,0:T(8,128)(2,1)} async-done(((bf16[512,2560]{1,0:T(8,128)(2,1)}), bf16[128,2560]{1,0:T(8,128)(2,1)}) %reduce-scatter.2.cloned.1.call-update) | async-done | bytes 655376 | tf_op jit(solution)/shard_map/reduce_scatter | solution.py:159
  (93 shorter events, 7.9 us)
Async XLA Ops:
  6.5 47.5 %copy-start = (bf16[2560,256]{1,0:T(8,128)(2,1)S(1)}, bf16[2560,256]{1,0:T(8,128)(2,1)}, u32[]{:S(2)}) copy-start(bf16[2560,256]{1,0:T(8,128)(2,1)} %param.15) | copy-start | bytes 3932164
  6.5 32.5 %copy-start.2 = (bf16[512,640]{1,0:T(8,128)(2,1)S(1)}, bf16[512,640]{1,0:T(8,128)(2,1)}, u32[]{:S(2)}) copy-start(bf16[512,640]{1,0:T(8,128)(2,1)} %param.12) | copy-start | bytes 1966084
  6.5 121.9 %all-gather.4.cloned.1.call-start = ((), (), s32[]{:S(2)}) async-start(), calls=%async_computation.2 | async-start | bytes 2949120 | tf_op jit(solution)/shard_map/all_gather | solution.py:72
  6.5 10.9 %collective-permute-start = (bf16[512,640]{1,0:T(8,128)(2,1)}, bf16[512,640]{1,0:T(8,128)(2,1)S(1)}, u32[]{:S(2)}, u32[]{:S(2)}) collective-permute-start(bf16[512,640]{1,0:T(8,128)(2,1)} %param.12), channel_id=1, source_target_pairs={{0,1},{1,2},{2,3},{3,0},{4,5},{5,6},{6,7},{7,4},{8,9},{9,10},{10,1... | collective-permute-start | bytes 1966088 | tf_op jit(solution)/shard_map/ppermute | solution.py:14
  17.5 10.0 %collective-permute-start.1 = (bf16[512,640]{1,0:T(8,128)(2,1)S(1)}, bf16[512,640]{1,0:T(8,128)(2,1)S(1)}, u32[]{:S(2)}, u32[]{:S(2)}) collective-permute-start(bf16[512,640]{1,0:T(8,128)(2,1)S(1)} %collective-permute-done), channel_id=1, source_target_pairs={{0,1},{1,2},{2,3},{3,0},{4,5},{5,6},{6,7},{7,4},{8,9},{9,10},{10,1... | collective-permute-start | bytes 1966088 | tf_op jit(solution)/shard_map/ppermute | solution.py:14
  27.5 10.1 %collective-permute-start.2 = (bf16[512,640]{1,0:T(8,128)(2,1)S(1)}, bf16[512,640]{1,0:T(8,128)(2,1)}, u32[]{:S(2)}, u32[]{:S(2)}) collective-permute-start(bf16[512,640]{1,0:T(8,128)(2,1)S(1)} %collective-permute-done.1), channel_id=1, source_target_pairs={{0,1},{1,2},{2,3},{3,0},{4,5},{5,6},{6,7},{7,4},{8,9},{9,10},{10,1... | collective-permute-start | bytes 1966088 | tf_op jit(solution)/shard_map/ppermute | solution.py:14
  39.2 4.1 %copy-start.9 = (bf16[2560,20]{0,1:T(8,128)(2,1)S(1)}, bf16[2560,20]{0,1:T(8,128)(2,1)}, u32[]{:S(2)}) copy-start(bf16[2560,20]{0,1:T(8,128)(2,1)} %param.16) | copy-start | bytes 307204
  39.2 4.1 %copy-start.14 = (f32[20]{0:T(128)S(1)}, f32[20]{0:T(128)}, u32[]{:S(2)}) copy-start(f32[20]{0:T(128)} %param.20) | copy-start | bytes 244
  39.3 4.1 %copy-start.15 = (f32[20]{0:T(128)S(1)}, f32[20]{0:T(128)}, u32[]{:S(2)}) copy-start(f32[20]{0:T(128)} %param.19) | copy-start | bytes 244
  41.0 2.3 %copy-start.4 = (bf16[512,5120]{1,0:T(8,128)(2,1)}, bf16[512,5120]{1,0:T(8,128)(2,1)S(1)}, u32[]{:S(2)}) copy-start(bf16[512,5120]{1,0:T(8,128)(2,1)S(1)} %constant_dynamic-update-slice_fusion) | copy-start | bytes 15728644
  45.5 8.6 %slice-start = ((s8[5242880]{0:T(1024)(128)(4,1)}), s8[1048576]{0:T(1024)(128)(4,1)S(1)}, s32[]{:S(2)}) async-start(s8[5242880]{0:T(1024)(128)(4,1)} %bitcast.69), calls=%async_computation.3 | async-start | bytes 2097152
  45.5 14.2 %copy-start.6 = (f32[3,8,2,128]{3,1,2,0:T(8,128)}, f32[3,8,2,128]{3,1,2,0:T(8,128)S(1)}, u32[]{:S(2)}) copy-start(f32[3,8,2,128]{3,1,2,0:T(8,128)S(1)} %copy.47) | copy-start | bytes 73732
  46.5 13.2 %copy-start.8 = (f32[3,8,2,128]{3,1,2,0:T(8,128)}, f32[3,8,2,128]{3,1,2,0:T(8,128)S(1)}, u32[]{:S(2)}) copy-start(f32[3,8,2,128]{3,1,2,0:T(8,128)S(1)} %copy.46) | copy-start | bytes 73732
  46.5 7.6 %slice-start.1 = ((s8[5242880]{0:T(1024)(128)(4,1)}), s8[4194304]{0:T(1024)(128)(4,1)S(1)}, s32[]{:S(2)}) async-start(s8[5242880]{0:T(1024)(128)(4,1)} %bitcast.69), calls=%async_computation.4 | async-start | bytes 8388608
  55.2 5.7 %collective-permute-start.3 = (bf16[3,1536]{1,0:T(4,128)(2,1)S(1)}, bf16[3,1536]{1,0:T(4,128)(2,1)S(1)}, u32[]{:S(2)}, u32[]{:S(2)}) collective-permute-start(bf16[3,1536]{1,0:T(4,128)(2,1)S(1)} %fusion.71), channel_id=1, source_target_pairs={{0,4},{4,8},{8,12},{12,16},{16,20},{20,24},{24,28},{1,5},{5,9},{9,... | collective-permute-start | bytes 27656 | tf_op jit(solution)/shard_map/ppermute | solution.py:23
  72.0 131.1 %reduce-scatter.2.cloned.1.call-start = ((), (), s32[]{:S(2)}) async-start(), calls=%async_computation.1 | async-start | bytes 3276800 | tf_op jit(solution)/shard_map/reduce_scatter | solution.py:159
  96.5 4.0 %copy-start.3 = (bf16[256,1280]{0,1:T(8,128)(2,1)S(1)}, bf16[256,1280]{0,1:T(8,128)(2,1)}, u32[]{:S(2)}) copy-start(bf16[256,1280]{0,1:T(8,128)(2,1)} %copy.39) | copy-start | bytes 1966084
  96.5 4.0 %copy-start.7 = (f32[3,8,2,128]{3,1,2,0:T(8,128)S(1)}, f32[3,8,2,128]{3,1,2,0:T(8,128)}, u32[]{:S(2)}) copy-start(f32[3,8,2,128]{3,1,2,0:T(8,128)} %copy-done.6) | copy-start | bytes 73732
  96.6 3.9 %copy-start.11 = (pred[256,256]{1,0:T(8,128)(4,1)S(1)}, pred[256,256]{1,0:T(8,128)(4,1)}, u32[]{:S(2)}) copy-start(pred[256,256]{1,0:T(8,128)(4,1)} %iota_compare_fusion) | copy-start | bytes 196612
  96.6 3.9 %copy-start.12 = (f32[20,256]{1,0:T(8,128)S(1)}, f32[20,256]{1,0:T(8,128)}, u32[]{:S(2)}) copy-start(f32[20,256]{1,0:T(8,128)} %get-tuple-element.16) | copy-start | bytes 61444
  128.5 5.8 %copy-start.5 = (f32[256,20,64]{0,2,1:T(8,128)S(1)}, f32[256,20,64]{0,2,1:T(8,128)}, u32[]{:S(2)}) copy-start(f32[256,20,64]{0,2,1:T(8,128)} %fusion.27) | copy-start | bytes 3932164
  128.5 5.8 %copy-start.10 = (f32[256,20]{0,1:T(8,128)S(1)}, f32[256,20]{0,1:T(8,128)}, u32[]{:S(2)}) copy-start(f32[256,20]{0,1:T(8,128)} %get-tuple-element.21) | copy-start | bytes 61444
  133.4 0.8 copy-start.1
  134.3 4.7 %copy-start.16 = (f32[20]{0:T(128)S(1)}, f32[20]{0:T(128)}, u32[]{:S(2)}) copy-start(f32[20]{0:T(128)} %get-tuple-element.22) | copy-start | bytes 244
  139.0 6.1 %copy-start.13 = (f32[1280]{0:T(1024)S(1)}, f32[1280]{0:T(1024)}, u32[]{:S(2)}) copy-start(f32[1280]{0:T(1024)} %mul.230) | copy-start | bytes 15364
  145.1 15.7 %copy-start.17 = (f32[1280]{0:T(1024)S(1)}, f32[1280]{0:T(1024)}, u32[]{:S(2)}) copy-start(f32[1280]{0:T(1024)} %param.22) | copy-start | bytes 15364
Sparse Core Ops, SparseCore 0:
  72.1 56.3 all-gather.3
  169.7 33.3 reduce-scatter.1
